TPU v7x, 32 devices: a whole 2x2x4 slice. The times are simulated.
32 devices in a mesh: grp: 2 (over y), row: 4 (over z), head: 2 (over x), br: 2 (over core).
Axes of the slice: x: 2, y: 2, z: 4, core: 2. Of those that a mesh axis runs over, the one named last changes fastest.
Arguments:
- pair_acts: float32 [16, 8, 128], P(('grp', 'row', 'head')), parts along dimension 0, may hold values from -6 to 6
- alignment: float32 [64, 8, 256], P(('grp', 'br'), ('row', 'head')), parts along dimension 0, may hold values from -6 to 6
- align_mask: int32 [64, 8], P('grp', ('row', 'head')), parts along dimension 0, may hold values from 0 to 1
- residue_mask: int32 [16], P('grp'), parts along dimension 0, may hold values from 0 to 1, as said below
- align_gain: float32 [256], replicated, may hold values from 0.25 to 1.75
- outer_in: float32 [256, 64], replicated, may hold values from -0.375 to 0.375
- outer_out: float32 [1024, 128], replicated, may hold values from -1 to 1
- tri_gain: float32 [2, 128], replicated, may hold values from 0.25 to 1.75
- tri_in: float32 [2, 128, 4, 128], P(None, None, 'br'), may hold values from -5 to 5
- tri_bias: float32 [2, 128, 4], P(None, None, 'br'), may hold values from -0.5 to 0.5
- tri_out: float32 [2, 4, 32, 128], P(None, 'br'), may hold values from -0.5 to 0.5
- pair_cotangent: float32 [16, 8, 128], P(('grp', 'row', 'head')), parts along dimension 0, may hold values from -6 to 6
Outputs:
- pair_out: float32 [16, 8, 128], P(('grp', 'row', 'head')), parts along dimension 0
- pair_grad: float32 [16, 8, 128], P(('grp', 'row', 'head')), parts along dimension 0
There are 2 independent parts, one for each index of `grp`. A program takes and returns all parts, laid end to end along the dimension named above; an argument that names none is the same for every part. Nothing has to cross between parts.
Inputs may be any that keep to these rules, and one draw needn't show every extreme that they name: `residue_mask`: 1 at residue 0, and 0 at one or more residues; `align_mask`: 1 at every residue of sequence 0 of each part.
All inputs are finite; a program needn't handle non-finite values.
Results may differ from a plain program's by a relative error of at most 0.0003.
Values sent between devices are 32-bit elements; how exact they have to be, the bound alone decides.
No kernel may reach another device: no remote copies, remote signals or barrier semaphores. Data moves between devices by JAX's collectives and lax.ppermute only.
A program may use at most 64 MiB of HBM per device.

v0:
```python
import jax
import jax.numpy as jnp
from jax import lax
from jax.sharding import PartitionSpec as P

OPC = 32
PRECISE = lax.Precision.HIGHEST
EPSILON = 1e-05
MASK_SHIFT = 1000000000.0


def normalize(values, scales):
    average = jnp.mean(values, axis=-1, keepdims=True)
    centred = values - average
    spread = jnp.mean(centred * centred, axis=-1, keepdims=True)
    return centred * lax.rsqrt(spread + EPSILON) * scales


def core_total(values):
    return lax.psum(values, "br")


def reorient(values):
    turned = jnp.swapaxes(values, 0, 1)
    return lax.all_to_all(turned, ("row", "head"), split_axis=0, concat_axis=1, tiled=True)


def prepare(values, scales, weight_in, weight_bias):
    normed = normalize(values, scales)
    projected = jnp.einsum("ijc,chd->ijhd", normed, weight_in, precision=PRECISE)
    bias_local = jnp.einsum("jkc,ch->hjk", normed, weight_bias, precision=PRECISE)
    return (projected, bias_local)


def attend(projected, bias_full, key_shift, weight_out):
    head_size = projected.shape[-1] // 4
    queries = projected[..., :head_size]
    key_proj = projected[..., head_size : 2 * head_size]
    value_proj = projected[..., 2 * head_size : 3 * head_size]
    gating = projected[..., 3 * head_size :]
    logits = jnp.einsum("ijhd,ikhd->ihjk", queries, key_proj, precision=PRECISE) * head_size ** (
        -0.5
    )
    logits = logits + bias_full[None] + key_shift
    attention = jax.nn.softmax(logits, axis=-1)
    attended = jnp.einsum("ihjk,ikhd->ijhd", attention, value_proj, precision=PRECISE)
    gated_out = jax.nn.sigmoid(gating) * attended
    return jnp.einsum("ijhd,hdc->ijc", gated_out, weight_out, precision=PRECISE)


def tri_forward(rows_in, scales, weight_in, weight_bias, weight_out, key_shift, pair_mask):

    def local_prep(values):
        return prepare(values, scales, weight_in, weight_bias)

    (projected, bias_local), pull_prep = jax.vjp(local_prep, rows_in)
    bias_full = lax.all_gather(bias_local, ("row", "head"), axis=1, tiled=True)

    def local_attend(proj_in, bias_in):
        return attend(proj_in, bias_in, key_shift, weight_out)

    partial_out, pull_attend = jax.vjp(local_attend, projected, bias_full)
    total_out = core_total(partial_out)
    return (rows_in + total_out * pair_mask, (pull_prep, pull_attend))


def tri_backward(grad_out, saved, pair_mask):
    pull_prep, pull_attend = saved
    grad_proj, grad_bias = pull_attend(grad_out * pair_mask)
    grad_local = lax.psum_scatter(grad_bias, ("row", "head"), scatter_dimension=1, tiled=True)
    (grad_rows,) = pull_prep((grad_proj, grad_local))
    return grad_out + core_total(grad_rows)


def body(
    pair_acts,
    alignment,
    align_mask,
    residue_mask,
    align_gain,
    outer_in,
    outer_out,
    tri_gain,
    tri_in,
    tri_bias,
    tri_out,
    pair_cotangent,
):
    row_count = pair_acts.shape[0]
    live = residue_mask.astype(jnp.float32)
    key_shift = (live - 1.0) * MASK_SHIFT
    row_live = lax.dynamic_slice_in_dim(
        live, lax.axis_index(("row", "head")) * row_count, row_count, 0
    )
    pair_mask = row_live[:, None, None] * live[None, :, None]
    seq_count = alignment.shape[0]
    mask_all = align_mask.astype(jnp.float32)
    mask_own = lax.dynamic_slice_in_dim(mask_all, lax.axis_index("br") * seq_count, seq_count, 0)
    normed = normalize(alignment, align_gain)
    projected = jnp.einsum("snc,ck->snk", normed, outer_in, precision=PRECISE)
    left_part = projected[..., :OPC] * mask_own[..., None]
    right_part = jnp.swapaxes(projected[..., OPC:] * mask_own[..., None], 1, 2)
    right_all, mask_cols = (
        lax.all_gather(right_part, ("row", "head"), axis=2, tiled=True),
        lax.all_gather(mask_all, ("row", "head"), axis=1, tiled=True),
    )
    counts = jnp.einsum("si,sj->ij", mask_all, mask_cols, precision=PRECISE)
    table = outer_out.reshape(OPC, OPC, outer_out.shape[-1])
    mixed_left = jnp.einsum("sip,pqc->siqc", left_part, table, precision=PRECISE)
    partial_outer = jnp.einsum("siqc,sqj->ijc", mixed_left, right_all, precision=PRECISE)
    outer_sum = core_total(partial_outer)
    pair_one = pair_acts + outer_sum / counts[..., None]
    pair_two, saved_start = tri_forward(
        pair_one, tri_gain[0], tri_in[0], tri_bias[0], tri_out[0], key_shift, pair_mask
    )
    turned_two = reorient(pair_two)
    turned_three, saved_end = tri_forward(
        turned_two, tri_gain[1], tri_in[1], tri_bias[1], tri_out[1], key_shift, pair_mask
    )
    pair_out = reorient(turned_three)
    grad_turned = reorient(pair_cotangent)
    grad_turned = tri_backward(grad_turned, saved_end, pair_mask)
    grad_two = reorient(grad_turned)
    pair_grad = tri_backward(grad_two, saved_start, pair_mask)
    return (pair_out, pair_grad)


def solution(mesh):
    in_specs = (
        P(("grp", "row", "head"), None, None),
        P(("grp", "br"), ("row", "head"), None),
        P("grp", ("row", "head")),
        P("grp"),
        P(),
        P(),
        P(),
        P(),
        P(None, None, "br", None),
        P(None, None, "br"),
        P(None, "br", None, None),
        P(("grp", "row", "head"), None, None),
    )
    out_specs = (P(("grp", "row", "head"), None, None), P(("grp", "row", "head"), None, None))
    return jax.shard_map(body, mesh=mesh, in_specs=in_specs, out_specs=out_specs, check_vma=False)
```

profile of v0, /device:TPU:0, one launch (start us, length us, event | category | flops | bytes accessed | tf_op | source)
XLA Modules:
  0.0 188.4 jit_solution(10134027815885279675)
XLA Ops:
  0.7 1.0 reduce_sum.121
  1.7 0.3 multiply_reduce_fusion
  2.0 0.7 convert_bitcast_fusion
  2.6 0.8 multiply_multiply_fusion
  3.7 32.3 %all_gather.12 = f32[16,32,8]{1,0,2:T(8,128)S(1)} all-gather(f32[16,32,1]{1,0,2:T(8,128)S(1)} %fusion.30), channel_id=1, replica_groups=mesh['grp'=2,'row'=4,'head'=2,'br'=2] {'row','head'}, dimensions={2}, use_global_device_ids=true | all-gather | bytes 18432 | tf_op jit(solution)/shard_map/all_gather | solution.py:104
  36.2 0.7 fusion.8
  36.9 0.7 convolution_bitcast_fusion.17
  37.6 2.5 %psum.35 = f32[1,8,128]{2,1,0:T(8,128)S(1)} all-reduce(f32[1,8,128]{2,1,0:T(8,128)S(1)} %convolution_bitcast_fusion.17), channel_id=1, replica_groups=mesh['grp'=2,'row'=4,'head'=2,'br'=2] {'br'}, use_global_device_ids=true, to_apply=%region_2.0 | all-reduce | flops 1024 | bytes 8192 | tf_op jit(solution)/shard_map/psum | solution.py:20
  40.0 20.4 %all-gather.2 = f32[8,1,32]{2,1,0:T(1,128)S(1)} all-gather(f32[1,1,32]{2,1,0:T(1,128)S(1)} %get-tuple-element.16), channel_id=1, replica_groups=mesh['grp'=2,'row'=4,'head'=2,'br'=2] {'row','head'}, dimensions={0}, use_global_device_ids=true | all-gather | bytes 1152 | tf_op jit(solution)/shard_map/all_gather | solution.py:105
  60.5 0.7 copy-done.8
  61.3 0.6 copy-done.7
  62.4 0.6 copy-done.9
  63.0 0.6 dynamic_slice.7
  63.6 0.6 broadcast_multiply_fusion.2
  64.5 0.5 copy-done.5
  65.1 16.3 %all-gather.3 = f32[8,8,2]{1,2,0:T(2,128)S(1)} all-gather(f32[1,8,2]{1,2,0:T(2,128)S(1)} %convolution_bitcast_fusion.19), channel_id=2, replica_groups=mesh['grp'=2,'row'=4,'head'=2,'br'=2] {'row','head'}, dimensions={0}, use_global_device_ids=true | all-gather | bytes 576 | tf_op jit(solution)/shard_map/all_gather | solution.py:57
  82.1 0.4 copy-done.2
  82.5 0.3 convolution_bitcast_fusion.16
  82.8 2.5 %psum.36 = f32[1,8,128]{2,1,0:T(8,128)S(1)} all-reduce(f32[1,8,128]{2,1,0:T(8,128)S(1)} %convolution_bitcast_fusion.16), channel_id=1, replica_groups=mesh['grp'=2,'row'=4,'head'=2,'br'=2] {'br'}, use_global_device_ids=true, to_apply=%region_7.0 | all-reduce | flops 1024 | bytes 8192 | tf_op jit(solution)/shard_map/psum | solution.py:20
  85.2 0.7 multiply_add_fusion
  85.9 3.3 %all-to-all-start = ((f32[8,1,128]{2,1,0:T(1,128)}), f32[8,1,128]{2,1,0:T(1,128)S(1)}, u32[]{:S(2)}, u32[]{:S(2)}) async-start(f32[8,1,128]{2,1,0:T(1,128)} %bitcast.32), calls=%async_computation | async-start | bytes 8192 | tf_op jit(solution)/shard_map/all_to_all | solution.py:25
  89.3 0.6 copy-done.10
  89.9 0.6 dynamic-slice
  90.5 5.1 %all-to-all-done = f32[8,1,128]{2,1,0:T(1,128)S(1)} async-done(((f32[8,1,128]{2,1,0:T(1,128)}), f32[8,1,128]{2,1,0:T(1,128)S(1)}, u32[]{:S(2)}, u32[]{:S(2)}) %all-to-all-start) | async-done | bytes 4128 | tf_op jit(solution)/shard_map/all_to_all | solution.py:25
  95.6 3.3 %all-to-all-start.2 = ((f32[8,1,128]{2,1,0:T(1,128)}), f32[8,1,128]{2,1,0:T(1,128)S(1)}, u32[]{:S(2)}, u32[]{:S(2)}) async-start(f32[8,1,128]{2,1,0:T(1,128)} %bitcast.54), calls=%async_computation.2 | async-start | bytes 8192 | tf_op jit(solution)/shard_map/all_to_all | solution.py:25
  99.5 20.9 %all-gather.4 = f32[8,8,2]{1,2,0:T(2,128)S(1)} all-gather(f32[1,8,2]{1,2,0:T(2,128)S(1)} %convolution_bitcast_fusion.18), channel_id=3, replica_groups=mesh['grp'=2,'row'=4,'head'=2,'br'=2] {'row','head'}, dimensions={0}, use_global_device_ids=true | all-gather | bytes 576 | tf_op jit(solution)/shard_map/all_gather | solution.py:57
  120.8 0.2 fusion.123
  121.7 0.3 multiply_reduce_fusion.2
  122.4 0.2 convolution_bitcast_fusion.6
  122.7 17.4 %all-reduce.8 = f32[2,8,8]{2,0,1:T(2,128)S(1)} all-reduce(f32[2,8,8]{2,0,1:T(2,128)S(1)} %copy.49), channel_id=4, replica_groups=mesh['grp'=2,'row'=4,'head'=2,'br'=2] {'row','head'}, use_global_device_ids=true, to_apply=%region_14.0.clone | all-reduce | flops 128 | bytes 1024
  140.0 0.8 fusion.92
  140.9 0.4 multiply_reduce_fusion.3
  141.6 2.5 %psum.38 = f32[1,8,128]{2,1,0:T(8,128)S(1)} all-reduce(f32[1,8,128]{2,1,0:T(8,128)S(1)} %add_bitcast_fusion), channel_id=1, replica_groups=mesh['grp'=2,'row'=4,'head'=2,'br'=2] {'br'}, use_global_device_ids=true, to_apply=%region_17.0 | all-reduce | flops 1024 | bytes 8192 | tf_op jit(solution)/shard_map/psum | solution.py:20
  144.0 0.6 bitcast_add_fusion.1
  144.6 3.3 %all-to-all-start.3 = ((f32[8,1,128]{2,1,0:T(1,128)}), f32[8,1,128]{2,1,0:T(1,128)S(1)}, u32[]{:S(2)}, u32[]{:S(2)}) async-start(f32[8,1,128]{2,1,0:T(1,128)} %bitcast.75), calls=%async_computation.3 | async-start | bytes 8192 | tf_op jit(solution)/shard_map/all_to_all | solution.py:25
  147.9 0.3 convolution_bitcast_fusion.15
  148.2 6.1 %all-to-all-done.3 = f32[8,1,128]{2,1,0:T(1,128)S(1)} async-done(((f32[8,1,128]{2,1,0:T(1,128)}), f32[8,1,128]{2,1,0:T(1,128)S(1)}, u32[]{:S(2)}, u32[]{:S(2)}) %all-to-all-start.3) | async-done | bytes 4128 | tf_op jit(solution)/shard_map/all_to_all | solution.py:25
  154.6 0.3 multiply_reduce_fusion.1
  155.3 0.2 convolution_bitcast_fusion.2
  155.6 17.9 %all-reduce.9 = f32[2,8,8]{2,0,1:T(2,128)S(1)} all-reduce(f32[2,8,8]{2,0,1:T(2,128)S(1)} %copy.52), channel_id=5, replica_groups=mesh['grp'=2,'row'=4,'head'=2,'br'=2] {'row','head'}, use_global_device_ids=true, to_apply=%region_19.0.clone | all-reduce | flops 128 | bytes 1024
  173.5 0.8 fusion.91
  174.4 0.4 fusion.65
  175.1 2.5 %all-reduce.10 = (f32[1,8,128]{2,1,0:T(8,128)S(1)}, f32[1,8,128]{2,1,0:T(8,128)S(1)}) all-reduce(f32[1,8,128]{2,1,0:T(8,128)S(1)} %convolution_bitcast_fusion.15, f32[1,8,128]{2,1,0:T(8,128)S(1)} %broadcast_add_fusion), channel_id=1, replica_groups=mesh['grp'=2,'row'=4,'head'=2,'br'=2] {'br'}, use_global_device_ids=true, to_apply=%region_12.0 | all-reduce | flops 2048 | bytes 16384 | tf_op jit(solution)/shard_map/psum | solution.py:20
  177.5 0.7 bitcast_add_fusion.2
  178.2 3.3 %all-to-all-start.1 = ((f32[8,1,128]{2,1,0:T(1,128)}), f32[8,1,128]{2,1,0:T(1,128)S(1)}, u32[]{:S(2)}, u32[]{:S(2)}) async-start(f32[8,1,128]{2,1,0:T(1,128)} %bitcast.52), calls=%async_computation.1 | async-start | bytes 8192 | tf_op jit(solution)/shard_map/all_to_all | solution.py:25
  181.5 0.6 bitcast_add_fusion
  182.1 5.8 %all-to-all-done.1 = f32[8,1,128]{2,1,0:T(1,128)S(1)} async-done(((f32[8,1,128]{2,1,0:T(1,128)}), f32[8,1,128]{2,1,0:T(1,128)S(1)}, u32[]{:S(2)}, u32[]{:S(2)}) %all-to-all-start.1) | async-done | bytes 4128 | tf_op jit(solution)/shard_map/all_to_all | solution.py:25
  187.9 0.6 copy.81
  (77 shorter events, 5.4 us)
Async XLA Ops:
  0.6 35.6 %copy-start = (f32[1024,128]{1,0:T(8,128)S(1)}, f32[1024,128]{1,0:T(8,128)}, u32[]{:S(2)}) copy-start(f32[1024,128]{1,0:T(8,128)} %param.18) | copy-start | bytes 1572868
  0.6 1.0 copy-start.3
  0.7 2.8 %copy-start.4 = (f32[256,64]{0,1:T(8,128)S(1)}, f32[256,64]{0,1:T(8,128)}, u32[]{:S(2)}) copy-start(f32[256,64]{0,1:T(8,128)} %param.17) | copy-start | bytes 196612
  36.9 24.4 %copy-start.1 = (f32[2,128,2,128]{3,2,1,0:T(2,128)S(1)}, f32[2,128,2,128]{3,2,1,0:T(2,128)}, u32[]{:S(2)}) copy-start(f32[2,128,2,128]{3,2,1,0:T(2,128)} %param.20) | copy-start | bytes 786436
  60.5 0.7 copy-start.8
  61.2 0.7 copy-start.7
  61.2 0.7 copy-start.6
  62.3 0.7 copy-start.9
  64.2 0.7 copy-start.5
  81.7 0.8 copy-start.2
  85.9 9.7 %all-to-all-start = ((f32[8,1,128]{2,1,0:T(1,128)}), f32[8,1,128]{2,1,0:T(1,128)S(1)}, u32[]{:S(2)}, u32[]{:S(2)}) async-start(f32[8,1,128]{2,1,0:T(1,128)} %bitcast.32), calls=%async_computation | async-start | bytes 8192 | tf_op jit(solution)/shard_map/all_to_all | solution.py:25
  89.2 0.7 copy-start.10
  95.6 25.7 %all-to-all-start.2 = ((f32[8,1,128]{2,1,0:T(1,128)}), f32[8,1,128]{2,1,0:T(1,128)S(1)}, u32[]{:S(2)}, u32[]{:S(2)}) async-start(f32[8,1,128]{2,1,0:T(1,128)} %bitcast.54), calls=%async_computation.2 | async-start | bytes 8192 | tf_op jit(solution)/shard_map/all_to_all | solution.py:25
  144.6 9.7 %all-to-all-start.3 = ((f32[8,1,128]{2,1,0:T(1,128)}), f32[8,1,128]{2,1,0:T(1,128)S(1)}, u32[]{:S(2)}, u32[]{:S(2)}) async-start(f32[8,1,128]{2,1,0:T(1,128)} %bitcast.75), calls=%async_computation.3 | async-start | bytes 8192 | tf_op jit(solution)/shard_map/all_to_all | solution.py:25
  178.2 9.7 %all-to-all-start.1 = ((f32[8,1,128]{2,1,0:T(1,128)}), f32[8,1,128]{2,1,0:T(1,128)S(1)}, u32[]{:S(2)}, u32[]{:S(2)}) async-start(f32[8,1,128]{2,1,0:T(1,128)} %bitcast.52), calls=%async_computation.1 | async-start | bytes 8192 | tf_op jit(solution)/shard_map/all_to_all | solution.py:25
where the time goes:
time: 189 us; the launch traced here: 188 us
  blocking collectives  135 us (71%)
  waiting for transfers between devices  17 us (9%)
  starting transfers between devices  13.2 us (7%)
  matrix products  8.39 us (4%)
  other arithmetic  7.59 us (4%)
  local copies, waits for them, and re-layouts  6.07 us (3%)
    all_gather x2, blocking collectives, tri_forward(): bias_full = lax.all_gather(bias_local, ('row', 'head'), axis=1, tiled=True)  37.2 us
    unnamed x2, blocking collectives  35.3 us
    all_gather x1, blocking collectives, body(): lax.all_gather(right_part, ('row', 'head'), axis=2, tiled=True)  32.3 us
    all_gather x1, blocking collectives, body(): lax.all_gather(mask_all, ('row', 'head'), axis=1, tiled=True)  20.4 us
    all_to_all x4, waiting for transfers between devices, reorient(): lax.all_to_all(turned, ('row', 'head'), split_axis=0, concat_axis=1, tile...  17 us
    all_to_all x4, starting transfers between devices, reorient(): lax.all_to_all(turned, ('row', 'head'), split_axis=0, concat_axis=1, tile...  13.2 us
    psum x4, blocking collectives, core_total(): return lax.psum(values, 'br')  9.82 us
    unnamed x26, local copies, waits for them, and re-layouts  4.8 us
  transfers between devices with their start and end apart: 4, of which 3 were waited for; matrix products, arithmetic and copies ran while one was open for 2% of the time, Pallas kernels for 0%

commit v1 on v0

--- a/solution.py
+++ b/solution.py
@@ -102,7 +102,7 @@
     right_part = jnp.swapaxes(projected[..., OPC:] * mask_own[..., None], 1, 2)
     right_all, mask_cols = (
         lax.all_gather(right_part, ("row", "head"), axis=2, tiled=True),
-        lax.all_gather(mask_all, ("row", "head"), axis=1, tiled=True),
+        jnp.concatenate(lax.all_gather(mask_all, ("row", "head")), axis=1),
     )
     counts = jnp.einsum("si,sj->ij", mask_all, mask_cols, precision=PRECISE)
     table = outer_out.reshape(OPC, OPC, outer_out.shape[-1])

time: 189 us -> 190 us (level)
    unnamed x2 -> x3, blocking collectives: 35.3 us -> 56.6 us
    all_gather x1 -> x0, blocking collectives: 20.4 us -> none  [body(): lax.all_gather(mask_all, ('row', 'head'), axis=1, tiled=True)]
    unnamed x26 -> x29, local copies, waits for them, and re-layouts: 4.8 us -> 4.17 us
  transfers between devices with their start and end apart: 4 -> 4, of which waited for: 3 -> 3; matrix products, arithmetic and copies ran while one was open for 2% -> 1% of each run, Pallas kernels for 0% -> 0%
where the time goes in v1:
time: 190 us; the launch traced here: 189 us
  blocking collectives  136 us (72%)
  waiting for transfers between devices  18.2 us (10%)
  starting transfers between devices  13.2 us (7%)
  matrix products  8.4 us (4%)
  other arithmetic  6.36 us (3%)
  local copies, waits for them, and re-layouts  5.52 us (3%)
    unnamed x3, blocking collectives  56.6 us
    all_gather x2, blocking collectives, tri_forward(): bias_full = lax.all_gather(bias_local, ('row', 'head'), axis=1, tiled=True)  37.2 us
    all_gather x1, blocking collectives, body(): lax.all_gather(right_part, ('row', 'head'), axis=2, tiled=True)  32.3 us
    all_to_all x4, waiting for transfers between devices, reorient(): lax.all_to_all(turned, ('row', 'head'), split_axis=0, concat_axis=1, tile...  18.2 us
    all_to_all x4, starting transfers between devices, reorient(): lax.all_to_all(turned, ('row', 'head'), split_axis=0, concat_axis=1, tile...  13.2 us
    psum x4, blocking collectives, core_total(): return lax.psum(values, 'br')  9.82 us
    unnamed x29, local copies, waits for them, and re-layouts  4.17 us
  transfers between devices with their start and end apart: 4, of which 3 were waited for; matrix products, arithmetic and copies ran while one was open for 1% of the time, Pallas kernels for 0%

profile of v1, /device:TPU:0, one launch (start us, length us, event | category | flops | bytes accessed | tf_op | source)
XLA Modules:
  0.0 189.5 jit_solution(7530111604733352308)
XLA Ops:
  0.7 1.0 reduce_sum.121
  1.7 0.3 multiply_reduce_fusion
  2.5 32.3 %all_gather.15 = f32[16,32,8]{1,0,2:T(8,128)S(1)} all-gather(f32[16,32,1]{1,0,2:T(8,128)S(1)} %fusion.30), channel_id=1, replica_groups=mesh['grp'=2,'row'=4,'head'=2,'br'=2] {'row','head'}, dimensions={2}, use_global_device_ids=true | all-gather | bytes 18432 | tf_op jit(solution)/shard_map/all_gather | solution.py:104
  34.9 0.7 fusion.8
  35.6 0.7 convolution_bitcast_fusion.17
  36.3 2.5 %psum.35 = f32[1,8,128]{2,1,0:T(8,128)S(1)} all-reduce(f32[1,8,128]{2,1,0:T(8,128)S(1)} %convolution_bitcast_fusion.17), channel_id=1, replica_groups=mesh['grp'=2,'row'=4,'head'=2,'br'=2] {'br'}, use_global_device_ids=true, to_apply=%region_2.0 | all-reduce | flops 1024 | bytes 8192 | tf_op jit(solution)/shard_map/psum | solution.py:20
  38.8 0.7 copy-done.7
  39.4 0.6 fusion.123
  40.8 21.3 %all-reduce.8 = f32[256]{0:T(256)S(1)} all-reduce(f32[256]{0:T(256)S(1)} %bitcast_dynamic-update-slice_fusion), channel_id=2, replica_groups=mesh['grp'=2,'row'=4,'head'=2,'br'=2] {'row','head'}, use_global_device_ids=true, to_apply=%add.8 | all-reduce | flops 256 | bytes 2048
  62.3 0.6 copy-done.9
  63.4 0.6 copy-done.11
  64.0 0.6 dynamic_slice.7
  64.6 0.6 broadcast_multiply_fusion.2
  65.5 0.5 copy-done.5
  66.1 16.3 %all-gather.3 = f32[8,8,2]{1,2,0:T(2,128)S(1)} all-gather(f32[1,8,2]{1,2,0:T(2,128)S(1)} %convolution_bitcast_fusion.19), channel_id=3, replica_groups=mesh['grp'=2,'row'=4,'head'=2,'br'=2] {'row','head'}, dimensions={0}, use_global_device_ids=true | all-gather | bytes 576 | tf_op jit(solution)/shard_map/all_gather | solution.py:57
  82.7 0.2 fusion.124
  82.9 0.2 convolution_bitcast_fusion.10
  83.2 0.4 copy-done.2
  83.5 0.3 convolution_bitcast_fusion.16
  83.8 2.5 %psum.36 = f32[1,8,128]{2,1,0:T(8,128)S(1)} all-reduce(f32[1,8,128]{2,1,0:T(8,128)S(1)} %convolution_bitcast_fusion.16), channel_id=1, replica_groups=mesh['grp'=2,'row'=4,'head'=2,'br'=2] {'br'}, use_global_device_ids=true, to_apply=%region_7.0 | all-reduce | flops 1024 | bytes 8192 | tf_op jit(solution)/shard_map/psum | solution.py:20
  86.3 0.7 multiply_add_fusion
  86.9 3.3 %all-to-all-start = ((f32[8,1,128]{2,1,0:T(1,128)}), f32[8,1,128]{2,1,0:T(1,128)S(1)}, u32[]{:S(2)}, u32[]{:S(2)}) async-start(f32[8,1,128]{2,1,0:T(1,128)} %bitcast.32), calls=%async_computation | async-start | bytes 8192 | tf_op jit(solution)/shard_map/all_to_all | solution.py:25
  90.3 6.4 %all-to-all-done = f32[8,1,128]{2,1,0:T(1,128)S(1)} async-done(((f32[8,1,128]{2,1,0:T(1,128)}), f32[8,1,128]{2,1,0:T(1,128)S(1)}, u32[]{:S(2)}, u32[]{:S(2)}) %all-to-all-start) | async-done | bytes 4128 | tf_op jit(solution)/shard_map/all_to_all | solution.py:25
  96.6 3.3 %all-to-all-start.2 = ((f32[8,1,128]{2,1,0:T(1,128)}), f32[8,1,128]{2,1,0:T(1,128)S(1)}, u32[]{:S(2)}, u32[]{:S(2)}) async-start(f32[8,1,128]{2,1,0:T(1,128)} %bitcast.54), calls=%async_computation.2 | async-start | bytes 8192 | tf_op jit(solution)/shard_map/all_to_all | solution.py:25
  100.5 20.9 %all-gather.4 = f32[8,8,2]{1,2,0:T(2,128)S(1)} all-gather(f32[1,8,2]{1,2,0:T(2,128)S(1)} %convolution_bitcast_fusion.18), channel_id=4, replica_groups=mesh['grp'=2,'row'=4,'head'=2,'br'=2] {'row','head'}, dimensions={0}, use_global_device_ids=true | all-gather | bytes 576 | tf_op jit(solution)/shard_map/all_gather | solution.py:57
  121.9 0.2 fusion.125
  122.2 0.2 convolution_bitcast_fusion.8
  122.7 0.3 multiply_reduce_fusion.2
  123.4 0.2 convolution_bitcast_fusion.6
  123.7 17.4 %all-reduce.9 = f32[2,8,8]{2,0,1:T(2,128)S(1)} all-reduce(f32[2,8,8]{2,0,1:T(2,128)S(1)} %copy.49), channel_id=5, replica_groups=mesh['grp'=2,'row'=4,'head'=2,'br'=2] {'row','head'}, use_global_device_ids=true, to_apply=%region_14.0.clone | all-reduce | flops 128 | bytes 1024
  141.1 0.8 fusion.93
  141.9 0.4 multiply_reduce_fusion.3
  142.6 2.5 %psum.38 = f32[1,8,128]{2,1,0:T(8,128)S(1)} all-reduce(f32[1,8,128]{2,1,0:T(8,128)S(1)} %add_bitcast_fusion), channel_id=1, replica_groups=mesh['grp'=2,'row'=4,'head'=2,'br'=2] {'br'}, use_global_device_ids=true, to_apply=%region_17.0 | all-reduce | flops 1024 | bytes 8192 | tf_op jit(solution)/shard_map/psum | solution.py:20
  145.0 0.6 bitcast_add_fusion.1
  145.6 3.3 %all-to-all-start.3 = ((f32[8,1,128]{2,1,0:T(1,128)}), f32[8,1,128]{2,1,0:T(1,128)S(1)}, u32[]{:S(2)}, u32[]{:S(2)}) async-start(f32[8,1,128]{2,1,0:T(1,128)} %bitcast.75), calls=%async_computation.3 | async-start | bytes 8192 | tf_op jit(solution)/shard_map/all_to_all | solution.py:25
  148.9 0.3 convolution_bitcast_fusion.15
  149.2 6.1 %all-to-all-done.3 = f32[8,1,128]{2,1,0:T(1,128)S(1)} async-done(((f32[8,1,128]{2,1,0:T(1,128)}), f32[8,1,128]{2,1,0:T(1,128)S(1)}, u32[]{:S(2)}, u32[]{:S(2)}) %all-to-all-start.3) | async-done | bytes 4128 | tf_op jit(solution)/shard_map/all_to_all | solution.py:25
  155.6 0.3 multiply_reduce_fusion.1
  156.4 0.2 convolution_bitcast_fusion.2
  156.6 17.9 %all-reduce.10 = f32[2,8,8]{2,0,1:T(2,128)S(1)} all-reduce(f32[2,8,8]{2,0,1:T(2,128)S(1)} %copy.52), channel_id=6, replica_groups=mesh['grp'=2,'row'=4,'head'=2,'br'=2] {'row','head'}, use_global_device_ids=true, to_apply=%region_19.0.clone | all-reduce | flops 128 | bytes 1024
  174.6 0.8 fusion.92
  175.4 0.4 fusion.66
  176.1 2.5 %all-reduce.11 = (f32[1,8,128]{2,1,0:T(8,128)S(1)}, f32[1,8,128]{2,1,0:T(8,128)S(1)}) all-reduce(f32[1,8,128]{2,1,0:T(8,128)S(1)} %convolution_bitcast_fusion.15, f32[1,8,128]{2,1,0:T(8,128)S(1)} %broadcast_add_fusion), channel_id=1, replica_groups=mesh['grp'=2,'row'=4,'head'=2,'br'=2] {'br'}, use_global_device_ids=true, to_apply=%region_12.0 | all-reduce | flops 2048 | bytes 16384 | tf_op jit(solution)/shard_map/psum | solution.py:20
  178.5 0.7 bitcast_add_fusion.2
  179.2 3.3 %all-to-all-start.1 = ((f32[8,1,128]{2,1,0:T(1,128)}), f32[8,1,128]{2,1,0:T(1,128)S(1)}, u32[]{:S(2)}, u32[]{:S(2)}) async-start(f32[8,1,128]{2,1,0:T(1,128)} %bitcast.52), calls=%async_computation.1 | async-start | bytes 8192 | tf_op jit(solution)/shard_map/all_to_all | solution.py:25
  182.5 0.6 bitcast_add_fusion
  183.1 5.8 %all-to-all-done.1 = f32[8,1,128]{2,1,0:T(1,128)S(1)} async-done(((f32[8,1,128]{2,1,0:T(1,128)}), f32[8,1,128]{2,1,0:T(1,128)S(1)}, u32[]{:S(2)}, u32[]{:S(2)}) %all-to-all-start.1) | async-done | bytes 4128 | tf_op jit(solution)/shard_map/all_to_all | solution.py:25
  188.9 0.6 copy.82
  (82 shorter events, 5.0 us)
Async XLA Ops:
  0.6 34.3 %copy-start = (f32[1024,128]{1,0:T(8,128)S(1)}, f32[1024,128]{1,0:T(8,128)}, u32[]{:S(2)}) copy-start(f32[1024,128]{1,0:T(8,128)} %param.18) | copy-start | bytes 1572868
  0.6 1.4 copy-start.10
  0.7 1.4 copy-start.8
  0.7 1.0 copy-start.3
  0.7 1.5 copy-start.4
  35.6 26.6 %copy-start.1 = (f32[2,128,2,128]{3,2,1,0:T(2,128)S(1)}, f32[2,128,2,128]{3,2,1,0:T(2,128)}, u32[]{:S(2)}) copy-start(f32[2,128,2,128]{3,2,1,0:T(2,128)} %param.20) | copy-start | bytes 786436
  38.7 0.7 copy-start.7
  62.3 0.7 copy-start.9
  62.3 0.7 copy-start.6
  63.3 0.7 copy-start.11
  65.3 0.7 copy-start.5
  82.7 0.8 copy-start.2
  86.9 9.7 %all-to-all-start = ((f32[8,1,128]{2,1,0:T(1,128)}), f32[8,1,128]{2,1,0:T(1,128)S(1)}, u32[]{:S(2)}, u32[]{:S(2)}) async-start(f32[8,1,128]{2,1,0:T(1,128)} %bitcast.32), calls=%async_computation | async-start | bytes 8192 | tf_op jit(solution)/shard_map/all_to_all | solution.py:25
  96.6 25.7 %all-to-all-start.2 = ((f32[8,1,128]{2,1,0:T(1,128)}), f32[8,1,128]{2,1,0:T(1,128)S(1)}, u32[]{:S(2)}, u32[]{:S(2)}) async-start(f32[8,1,128]{2,1,0:T(1,128)} %bitcast.54), calls=%async_computation.2 | async-start | bytes 8192 | tf_op jit(solution)/shard_map/all_to_all | solution.py:25
  145.6 9.7 %all-to-all-start.3 = ((f32[8,1,128]{2,1,0:T(1,128)}), f32[8,1,128]{2,1,0:T(1,128)S(1)}, u32[]{:S(2)}, u32[]{:S(2)}) async-start(f32[8,1,128]{2,1,0:T(1,128)} %bitcast.75), calls=%async_computation.3 | async-start | bytes 8192 | tf_op jit(solution)/shard_map/all_to_all | solution.py:25
  179.2 9.7 %all-to-all-start.1 = ((f32[8,1,128]{2,1,0:T(1,128)}), f32[8,1,128]{2,1,0:T(1,128)S(1)}, u32[]{:S(2)}, u32[]{:S(2)}) async-start(f32[8,1,128]{2,1,0:T(1,128)} %bitcast.52), calls=%async_computation.1 | async-start | bytes 8192 | tf_op jit(solution)/shard_map/all_to_all | solution.py:25
